TPU v7x, 1024 devices: a whole 4x4x32 slice. The times are simulated.
1024 devices in a mesh: energy: 64 (over z, core), ribbon: 16 (over y, x).
Axes of the slice: x: 4, y: 4, z: 32, core: 2. Of those that a mesh axis runs over, the one named last changes fastest.
Arguments:
- transfer: float32 [64, 16, 2, 256, 256], P('energy', 'ribbon'), may hold values from -1.25 to 1.25
- source: float32 [64, 16, 2, 256, 256], P('energy', 'ribbon'), may hold values from -6 to 6
- coulomb: float32 [16, 256, 256], P('ribbon'), may hold values from -6 to 6
Outputs:
- lesser: float32 [64, 16, 2, 256, 256], P('energy', 'ribbon')
- screened: float32 [64, 16, 2, 256, 256], P('energy', 'ribbon')
All inputs are finite; a program needn't handle non-finite values.
Results may differ from a plain program's by a relative error of at most 0.0001.
Values sent between devices are 32-bit elements; how exact they have to be, the bound alone decides.
No kernel may reach another device: no remote copies, remote signals or barrier semaphores. Data moves between devices by JAX's collectives and lax.ppermute only.
A program may use at most 64 MiB of HBM per device.

v0:
```python
import math

import jax
import jax.numpy as jnp
import numpy as np
from jax import lax
from jax.experimental import pallas as pl
from jax.experimental.pallas import tpu as pltpu
from jax.sharding import Mesh
from jax.sharding import PartitionSpec as P


F32 = jnp.float32
BF16 = jnp.bfloat16
STAGGER = 4500
VMEM = pl.BlockSpec(memory_space=pltpu.VMEM)


def split(value):
    high = value.astype(BF16)
    return high, (value - high.astype(F32)).astype(BF16)


def put(slot, re, im):
    for n, value in enumerate((re, im, re + im, re - im)):
        slot[n, 0], slot[n, 1] = split(value)


def left(slot, n):
    return jnp.concatenate([slot[n, 0], slot[n, 0], slot[n, 1]], axis=1)


def right(slot, n):
    return jnp.concatenate([slot[n, 0], slot[n, 1], slot[n, 0]], axis=0)


def right_t(slot, n):
    return jnp.concatenate([slot[n, 0], slot[n, 1], slot[n, 0]], axis=1)


def dot(a, b):
    return jnp.dot(a, b, preferred_element_type=F32)


def dot_t(a, b):
    return lax.dot_general(a, b, (((1,), (1,)), ((), ())), preferred_element_type=F32)


def times(a, b):
    p1 = dot(left(a, 0), right(b, 0))
    p2 = dot(left(a, 1), right(b, 1))
    p3 = dot(left(a, 2), right(b, 2))
    return p1 - p2, p3 - p1 - p2


def times_adjoint(a, b):
    p1 = dot_t(left(a, 0), right_t(b, 0))
    p2 = dot_t(left(a, 1), right_t(b, 1))
    p3 = dot_t(left(a, 2), right_t(b, 3))
    return p1 + p2, p3 - p1 + p2


def sandwich(a, b, mid):
    put(mid, *times(a, b))
    return times_adjoint(mid, a)


def run(body, outs, scratch, flops, *args):
    many = isinstance(outs, (list, tuple))
    return pl.pallas_call(
        body,
        out_shape=outs,
        in_specs=[VMEM] * len(args),
        out_specs=[VMEM] * len(outs) if many else VMEM,
        scratch_shapes=scratch,
        compiler_params=pltpu.CompilerParams(vmem_limit_bytes=24 * 1024 * 1024),
        cost_estimate=pl.CostEstimate(flops=flops, bytes_accessed=4 << 20, transcendentals=0),
    )(*args)


def row_map(own, prev, opp_re, opp_im, nxt, order, prefix, total, late, *slots):
    x = lax.axis_index("ribbon_1")
    for r, ref in ((0, own), (1, prev), (3, nxt)):
        order[lax.rem(x + 4 - r, 4)] = ref[...]
    across = lax.rem(x + 2, 4)
    order[across, 0] = opp_re[...]
    order[across, 1] = opp_im[...]
    a0, a1, a2, a3, pair, upper = slots
    for j, slot in ((0, a0), (1, a1), (2, a2), (3, a3)):
        put(slot, order[j, 0], order[j, 1])
    low_re, low_im = times(a1, a0)
    up_re, up_im = times(a3, a2)
    put(pair, low_re, low_im)
    put(upper, up_re, up_im)
    late[0], late[1] = up_re, up_im
    total[0], total[1] = times(upper, pair)

    @pl.when(x == 0)
    def _():
        prefix[...] = own[...]

    @pl.when(x == 1)
    def _():
        prefix[0], prefix[1] = low_re, low_im

    @pl.when(x == 2)
    def _():
        prefix[0], prefix[1] = times(a2, pair)

    @pl.when(x == 3)
    def _():
        prefix[...] = total[...]


def row_add(order, late, own, prev, opp_re, opp_im, nxt, prefix, total, adds, *slots):
    x = lax.axis_index("ribbon_1")
    for r, ref in ((0, own), (1, prev), (3, nxt)):
        adds[lax.rem(x + 4 - r, 4)] = ref[...]
    across = lax.rem(x + 2, 4)
    adds[across, 0] = opp_re[...]
    adds[across, 1] = opp_im[...]
    a, b, c, d, mid, mid2 = slots
    put(a, order[1, 0], order[1, 1])
    put(b, adds[0, 0], adds[0, 1])
    put(c, order[3, 0], order[3, 1])
    put(d, adds[2, 0], adds[2, 1])
    low_re, low_im = sandwich(a, b, mid)
    low_re, low_im = low_re + adds[1, 0], low_im + adds[1, 1]
    up_re, up_im = sandwich(c, d, mid2)
    put(b, low_re, low_im)
    put(d, late[0], late[1])
    tot_re, tot_im = sandwich(d, b, mid)
    total[0] = tot_re + (up_re + adds[3, 0])
    total[1] = tot_im + (up_im + adds[3, 1])

    @pl.when(x == 0)
    def _():
        prefix[...] = own[...]

    @pl.when(x == 1)
    def _():
        prefix[0], prefix[1] = low_re, low_im

    @pl.when(x == 2)
    def _():
        put(a, order[2, 0], order[2, 1])
        own_re, own_im = sandwich(a, b, mid2)
        prefix[0], prefix[1] = own_re + adds[2, 0], own_im + adds[2, 1]

    @pl.when(x == 3)
    def _():
        prefix[...] = total[...]


def join_rows(pre_map, pre_add, tot_map, tot_add, got_map, got_add, joint, new_map, *slots):
    y = lax.axis_index("ribbon_0")
    a, b, mid = slots

    @pl.when(y == 0)
    def _():
        put(a, got_map[0], got_map[1])
        put(b, tot_add[0], tot_add[1])
        joint[...] = got_add[...]
        new_map[...] = pre_map[...]

    @pl.when(y == 1)
    def _():
        put(a, tot_map[0], tot_map[1])
        put(b, got_add[0], got_add[1])
        joint[...] = tot_add[...]
        new_map[...] = pre_map[...]

    @pl.when(y == 3)
    def _():
        put(b, got_map[0], got_map[1])
        put(a, pre_map[0], pre_map[1])
        new_map[0], new_map[1] = times(a, b)
        put(b, got_add[0], got_add[1])
        joint[...] = pre_add[...]

    @pl.when(y != 2)
    def _():
        re, im = sandwich(a, b, mid)
        joint[0] += re
        joint[1] += im

    @pl.when(y == 2)
    def _():
        joint[...] = pre_add[...]
        new_map[...] = pre_map[...]


def finish_chain(pre_add, joint, new_map, got_add, passed, lesser, keep, send, a, b, mid):
    y = lax.axis_index("ribbon_0")
    c = lax.axis_index("energy_1")
    count, rows = keep.shape[0], keep.shape[2]

    @pl.when(y == 0)
    def _():
        lesser[...] = pre_add[...]

    @pl.when(y == 1)
    def _():
        put(b, got_add[0], got_add[1])
        lesser[...] = pre_add[...]

    @pl.when(y > 1)
    def _():
        put(b, passed[0], passed[1])
        lesser[...] = joint[...]

    @pl.when(y > 0)
    def _():
        put(a, new_map[0], new_map[1])
        re, im = sandwich(a, b, mid)
        lesser[0] += re
        lesser[1] += im

    for p in range(2):
        for half, out in ((c, keep), (1 - c, send)):
            part = lesser[p, :, pl.ds(pl.multiple_of(half * 128, 128), 128)]
            out[:, p] = part.reshape(count, rows, 128)


def pack(keep, got, groups, idle):
    c = lax.axis_index("energy_1")
    groups[:, c] = keep[...]
    groups[:, 1 - c] = got[...]

    @pl.when(c == 1)
    def _():
        idle[...] = keep[0, 0]
        idle[...] = lax.fori_loop(0, STAGGER, lambda _, v: v * 0.5 + 1.0, idle[...])


def correlate(forward, backward, given, out, terms):
    length = forward.shape[0] // 2
    count = length // 4
    rows = given.shape[0] // (4 * count)
    for r in range(rows):
        lanes = slice(r * 128, (r + 1) * 128)
        for n in range(4):
            high, low = split(given[pl.ds(n * rows + r, count, stride=4 * rows), :])
            terms[0, n * count : (n + 1) * count, lanes] = high
            terms[1, n * count : (n + 1) * count, lanes] = low
    table = forward[...]
    back = backward[...]
    for n in range(rows // 2):
        lanes = slice(n * 256, (n + 1) * 256)
        high, low = terms[0, :, lanes], terms[1, :, lanes]
        spec = dot(table, jnp.concatenate([high, low, high], axis=0))
        power = spec[:length] * spec[:length] + spec[length:] * spec[length:]
        high, low = split(power)
        lag = dot(back, jnp.concatenate([high, low, high], axis=0))
        for q in range(2):
            for k in range(4):
                out[pl.ds(k * rows + 2 * n + q, count, stride=4 * rows), :] = lag[
                    k * count : (k + 1) * count, q * 128 : (q + 1) * 128
                ]


def screen(bare, mine, theirs, out, both):
    c = lax.axis_index("energy_1")
    order = bare.shape[0]
    high, low = split(bare[...])
    wide = jnp.concatenate([high, high, low], axis=1)
    wide_t = jnp.concatenate([high, low, high], axis=1)
    own = [mine[:, c, p].reshape(order, 128) for p in range(2)]
    other = [theirs[:, p].reshape(order, 128) for p in range(2)]
    for at, parts in ((c, own), (1 - c, other)):
        high, low = split(jnp.concatenate(parts, axis=1))
        half = dot(wide, jnp.concatenate([high, low, high], axis=0))
        both[at, 0] = half[:, :128]
        both[at, 1] = half[:, 128:]
    for p in range(2):
        high, low = split(jnp.concatenate([both[0, p], both[1, p]], axis=1))
        full = dot_t(jnp.concatenate([high, high, low], axis=1), wide_t) * (1.0 / order)
        out[p] = bare[...] + full if p == 0 else full


def tables(energies):
    length = 2 * energies

    def terms(table):
        high = table.astype(BF16)
        low = (table - high.astype(np.float64)).astype(BF16)
        return np.concatenate([high, high, low], axis=1)

    freq = np.arange(length)
    point = np.arange(energies)
    phase = 2.0 * math.pi / length * (np.outer(freq, point) % length)
    cosine, sine = np.cos(phase), np.sin(phase)
    columns, rows = [], []
    for parity in range(2):
        co, si = cosine[:, parity::2], sine[:, parity::2]
        columns += [np.concatenate([co, -si], axis=0), np.concatenate([si, co], axis=0)]
        rows += [co.T, si.T]
    forward = terms(np.concatenate(columns, axis=1))
    backward = terms(np.concatenate(rows, axis=0) / (length * energies))
    return jnp.asarray(forward), jnp.asarray(backward)


def shift(value, axis, step):
    length = lax.axis_size(axis)
    return lax.ppermute(value, axis, [(i, (i + step) % length) for i in range(length)])


def gather_row(value):
    prev, nxt = shift(value, "ribbon_1", 1), shift(value, "ribbon_1", -1)
    return prev, nxt


def step(transfer, source, coulomb):
    a, b, bare = transfer[0, 0], source[0, 0], coulomb[0]
    order = a.shape[-1]
    count = lax.axis_size("energy_0")
    rows = order // count
    matrix = jax.ShapeDtypeStruct((2, order, order), F32)
    slot = pltpu.VMEM((4, 2, order, order), BF16)
    product = 18 * order**3

    a_prev, a_next = gather_row(a)
    b_prev, b_next = gather_row(b)
    a_opp_re = shift(a_prev[0], "ribbon_1", 1)
    a_opp_im = shift(a_next[1], "ribbon_1", -1)
    b_opp_re = shift(b_prev[0], "ribbon_1", 1)
    b_opp_im = shift(b_next[1], "ribbon_1", -1)

    four = jax.ShapeDtypeStruct((4, 2, order, order), F32)
    maps, pre_map, tot_map, late = run(
        row_map, [four, matrix, matrix, matrix], [slot] * 6, 4 * product,
        a, a_prev, a_opp_re, a_opp_im, a_next,
    )
    got_map = lax.ppermute(tot_map, "ribbon_0", [(1, 0), (2, 3)])
    pre_add, tot_add = run(
        row_add, [matrix, matrix], [pltpu.VMEM((4, 2, order, order), F32)] + [slot] * 6,
        8 * product,
        maps, late, b, b_prev, b_opp_re, b_opp_im, b_next,
    )
    got_add = lax.ppermute(tot_add, "ribbon_0", [(0, 1), (1, 0), (2, 3)])
    joint, new_map = run(
        join_rows, [matrix, matrix], [slot] * 3, 3 * product,
        pre_map, pre_add, tot_map, tot_add, got_map, got_add,
    )
    passed = lax.ppermute(joint, "ribbon_0", [(1, 2), (0, 3)])
    half = jax.ShapeDtypeStruct((count, 2, rows, 128), F32)
    lesser, keep, send = run(
        finish_chain, [matrix, half, half], [slot] * 3, 2 * product,
        pre_add, joint, new_map, got_add, passed,
    )

    c = lax.axis_index("energy_1")
    swap = [(0, 1), (1, 0)]
    groups = run(
        pack, jax.ShapeDtypeStruct((count, 2, 2, rows, 128), F32),
        [pltpu.VMEM((rows, 128), F32)], product,
        keep, lax.ppermute(send, "energy_1", swap),
    )
    turned = lax.all_to_all(groups.reshape(count, 4 * rows, 128), "energy_0", 0, 0, tiled=True)
    forward, backward = tables(2 * count)
    lags = run(
        correlate, jax.ShapeDtypeStruct((4 * count * rows, 128), F32),
        [pltpu.VMEM((2, 4 * count, rows * 128), BF16)], 4 * product,
        forward, backward, turned.reshape(-1, 128),
    )
    returned = lax.all_to_all(lags.reshape(count, 4 * rows, 128), "energy_0", 0, 0, tiled=True)
    returned = returned.reshape(count, 2, 2, rows, 128)
    other_lag = lax.dynamic_index_in_dim(returned, 1 - c, 1, keepdims=False)
    halves = lax.ppermute(other_lag, "energy_1", swap)
    screened = run(
        screen, matrix, [pltpu.VMEM((2, 2, order, 128), F32)], product,
        bare, returned, halves,
    )
    return (lesser[None, None], screened[None, None])


def solution(mesh):
    sizes = (mesh.shape["energy"] // 2, 2, 4, 4)
    names = ("energy_0", "energy_1", "ribbon_0", "ribbon_1")
    split_mesh = Mesh(mesh.devices.reshape(sizes), names)
    energy, ribbon = names[:2], names[2:]
    in_specs = (
        P(energy, ribbon, None, None, None),
        P(energy, ribbon, None, None, None),
        P(ribbon, None, None),
    )
    out_specs = (P(energy, ribbon, None, None, None), P(energy, ribbon, None, None, None))
    return jax.shard_map(
        step, mesh=split_mesh, in_specs=in_specs, out_specs=out_specs, check_vma=False
    )
```

profile of v0, /device:TPU:29, one launch (start us, length us, event | category | flops | bytes accessed | tf_op | source)
XLA Modules:
  0.0 242.6 jit_solution(3249780191094949999)
XLA Ops:
  0.6 3.0 %collective-permute-start = (f32[2,256,256]{2,1,0:T(8,128)}, f32[2,256,256]{2,1,0:T(8,128)S(1)}, u32[]{:S(2)}, u32[]{:S(2)}) collective-permute-start(f32[2,256,256]{2,1,0:T(8,128)} %bitcast.24), channel_id=1, source_target_pairs={{0,1},{1,2},{2,3},{3,0},{4,5},{5,6},{6,7},{7,4},{8,9},{9,10},{10,1... | collective-permute-start | bytes 1572872 | tf_op jit(solution)/shard_map/ppermute | solution.py:305
  3.6 2.5 %collective-permute-start.2 = (f32[2,256,256]{2,1,0:T(8,128)}, f32[2,256,256]{2,1,0:T(8,128)S(1)}, u32[]{:S(2)}, u32[]{:S(2)}) collective-permute-start(f32[2,256,256]{2,1,0:T(8,128)} %bitcast.25), channel_id=1, source_target_pairs={{0,3},{1,0},{2,1},{3,2},{4,7},{5,4},{6,5},{7,6},{8,11},{9,8},{10,9... | collective-permute-start | bytes 1572872 | tf_op jit(solution)/shard_map/ppermute | solution.py:305
  6.1 2.8 %collective-permute-start.4 = (f32[2,256,256]{2,1,0:T(8,128)}, f32[2,256,256]{2,1,0:T(8,128)S(1)}, u32[]{:S(2)}, u32[]{:S(2)}) collective-permute-start(f32[2,256,256]{2,1,0:T(8,128)} %bitcast.27), channel_id=1, source_target_pairs={{0,1},{1,2},{2,3},{3,0},{4,5},{5,6},{6,7},{7,4},{8,9},{9,10},{10,1... | collective-permute-start | bytes 1572872 | tf_op jit(solution)/shard_map/ppermute | solution.py:305
  8.9 2.5 %collective-permute-start.6 = (f32[2,256,256]{2,1,0:T(8,128)}, f32[2,256,256]{2,1,0:T(8,128)S(1)}, u32[]{:S(2)}, u32[]{:S(2)}) collective-permute-start(f32[2,256,256]{2,1,0:T(8,128)} %bitcast.28), channel_id=1, source_target_pairs={{0,3},{1,0},{2,1},{3,2},{4,7},{5,4},{6,5},{7,6},{8,11},{9,8},{10,9... | collective-permute-start | bytes 1572872 | tf_op jit(solution)/shard_map/ppermute | solution.py:305
  11.4 4.3 %collective-permute-done.prev = f32[2,256,256]{2,1,0:T(8,128)S(1)} collective-permute-done((f32[2,256,256]{2,1,0:T(8,128)}, f32[2,256,256]{2,1,0:T(8,128)S(1)}, u32[]{:S(2)}, u32[]{:S(2)}) %collective-permute-start) | collective-permute-done | bytes 524320 | tf_op jit(solution)/shard_map/ppermute | solution.py:305
  15.7 2.8 %collective-permute-start.1 = (f32[256,256]{1,0:T(8,128)S(1)}, f32[256,256]{1,0:T(8,128)S(1)}, u32[]{:S(2)}, u32[]{:S(2)}) collective-permute-start(f32[256,256]{1,0:T(8,128)S(1)} %slice_bitcast_fusion.3), channel_id=1, source_target_pairs={{0,1},{1,2},{2,3},{3,0},{4,5},{5,6},{6,7},{7,4},{8,9},{9,10},{10,1... | collective-permute-start | bytes 786440 | tf_op jit(solution)/shard_map/ppermute | solution.py:305
  18.6 2.5 %collective-permute-start.3 = (f32[256,256]{1,0:T(8,128)S(1)}, f32[256,256]{1,0:T(8,128)S(1)}, u32[]{:S(2)}, u32[]{:S(2)}) collective-permute-start(f32[256,256]{1,0:T(8,128)S(1)} %slice_bitcast_fusion.2), channel_id=1, source_target_pairs={{0,3},{1,0},{2,1},{3,2},{4,7},{5,4},{6,5},{7,6},{8,11},{9,8},{10,9... | collective-permute-start | bytes 786440 | tf_op jit(solution)/shard_map/ppermute | solution.py:305
  21.0 5.9 %collective-permute-done.4.prev = f32[2,256,256]{2,1,0:T(8,128)S(1)} collective-permute-done((f32[2,256,256]{2,1,0:T(8,128)}, f32[2,256,256]{2,1,0:T(8,128)S(1)}, u32[]{:S(2)}, u32[]{:S(2)}) %collective-permute-start.4) | collective-permute-done | bytes 524320 | tf_op jit(solution)/shard_map/ppermute | solution.py:305
  26.9 2.8 %collective-permute-start.5 = (f32[256,256]{1,0:T(8,128)S(1)}, f32[256,256]{1,0:T(8,128)S(1)}, u32[]{:S(2)}, u32[]{:S(2)}) collective-permute-start(f32[256,256]{1,0:T(8,128)S(1)} %slice_bitcast_fusion.1), channel_id=1, source_target_pairs={{0,1},{1,2},{2,3},{3,0},{4,5},{5,6},{6,7},{7,4},{8,9},{9,10},{10,1... | collective-permute-start | bytes 786440 | tf_op jit(solution)/shard_map/ppermute | solution.py:305
  29.8 2.6 %collective-permute-start.7 = (f32[256,256]{1,0:T(8,128)S(1)}, f32[256,256]{1,0:T(8,128)S(1)}, u32[]{:S(2)}, u32[]{:S(2)}) collective-permute-start(f32[256,256]{1,0:T(8,128)S(1)} %slice_bitcast_fusion), channel_id=1, source_target_pairs={{0,3},{1,0},{2,1},{3,2},{4,7},{5,4},{6,5},{7,6},{8,11},{9,8},{10,9... | collective-permute-start | bytes 786440 | tf_op jit(solution)/shard_map/ppermute | solution.py:305
  32.5 2.6 %collective-permute-done.3.opp_im = f32[256,256]{1,0:T(8,128)S(1)} collective-permute-done((f32[256,256]{1,0:T(8,128)S(1)}, f32[256,256]{1,0:T(8,128)S(1)}, u32[]{:S(2)}, u32[]{:S(2)}) %collective-permute-start.3) | collective-permute-done | bytes 262176 | tf_op jit(solution)/shard_map/ppermute | solution.py:305
  35.1 2.0 shard_map.68
  38.2 2.5 %collective-permute-done.7.opp_im = f32[256,256]{1,0:T(8,128)S(1)} collective-permute-done((f32[256,256]{1,0:T(8,128)S(1)}, f32[256,256]{1,0:T(8,128)S(1)}, u32[]{:S(2)}, u32[]{:S(2)}) %collective-permute-start.7) | collective-permute-done | bytes 262176 | tf_op jit(solution)/shard_map/ppermute | solution.py:305
  40.7 3.6 %shard_map.69 = (f32[2,256,256]{2,1,0:T(8,128)S(1)}, f32[2,256,256]{2,1,0:T(8,128)S(1)}) custom-call(f32[4,2,256,256]{3,2,1,0:T(8,128)S(1)} %get-tuple-element.13.order, f32[2,256,256]{2,1,0:T(8,128)S(1)} %get-tuple-element.14.late, f32[2,256,256]{2,1,0:T(8,128)S(1)} %bitcast.29, f32[2,256,256]{2,1,0:T(8,128)S(1)} %collective-permute-done.4.prev, ...), custom_call_target="tpu_custom_call" | custom-call | flops 2415919104 | bytes 4194304 | tf_op jit(solution)/shard_map/pallas_call | solution.py:70
  44.2 1.3 collective-permute-start.9
  45.5 1.3 collective-permute-start.8
  46.8 10.9 %collective-permute-done.9.got_add = f32[2,256,256]{2,1,0:T(8,128)S(1)} collective-permute-done((f32[2,256,256]{2,1,0:T(8,128)S(1)}, f32[2,256,256]{2,1,0:T(8,128)S(1)}, u32[]{:S(2)}, u32[]{:S(2)}) %collective-permute-start.9) | collective-permute-done | bytes 524320 | tf_op jit(solution)/shard_map/ppermute | solution.py:340
  57.8 11.2 %collective-permute-done.8.got_map = f32[2,256,256]{2,1,0:T(8,128)S(1)} collective-permute-done((f32[2,256,256]{2,1,0:T(8,128)S(1)}, f32[2,256,256]{2,1,0:T(8,128)S(1)}, u32[]{:S(2)}, u32[]{:S(2)}) %collective-permute-start.8) | collective-permute-done | bytes 524320 | tf_op jit(solution)/shard_map/ppermute | solution.py:334
  69.0 1.5 shard_map.70
  70.5 1.3 collective-permute-start.10
  71.8 12.6 %collective-permute-done.10.passed = f32[2,256,256]{2,1,0:T(8,128)S(1)} collective-permute-done((f32[2,256,256]{2,1,0:T(8,128)S(1)}, f32[2,256,256]{2,1,0:T(8,128)S(1)}, u32[]{:S(2)}, u32[]{:S(2)}) %collective-permute-start.10) | collective-permute-done | bytes 524320 | tf_op jit(solution)/shard_map/ppermute | solution.py:345
  84.4 1.8 shard_map.71
  86.2 5.5 %collective-permute-start.11 = (f32[32,2,8,128]{3,2,1,0:T(8,128)S(1)}, f32[32,2,8,128]{3,2,1,0:T(8,128)S(1)}, u32[]{:S(2)}, u32[]{:S(2)}) collective-permute-start(f32[32,2,8,128]{3,2,1,0:T(8,128)S(1)} %get-tuple-element.23), channel_id=1, source_target_pairs={{0,16},{16,0},{1,17},{17,1},{2,18},{18,2},{3,19},{19,3},{4,20},{20... | collective-permute-start | bytes 786440 | tf_op jit(solution)/shard_map/ppermute | solution.py:357
  91.7 1.1 collective-permute-done.11.got
  92.8 23.7 %shard_map.72 = f32[32,2,2,8,128]{4,3,2,1,0:T(8,128)S(1)} custom-call(f32[32,2,8,128]{3,2,1,0:T(8,128)S(1)} %get-tuple-element.22.keep, f32[32,2,8,128]{3,2,1,0:T(8,128)S(1)} %collective-permute-done.11.got), custom_call_target="tpu_custom_call" | custom-call | flops 301989888 | bytes 4194304 | tf_op jit(solution)/shard_map/pallas_call | solution.py:70
  116.5 70.3 %all_to_all.10 = f32[32,32,128]{2,1,0:T(8,128)S(1)} all-to-all(f32[32,32,128]{2,1,0:T(8,128)S(1)} %bitcast.22), channel_id=1, replica_groups=mesh['energy_0'=32,'energy_1'=2,'ribbon_0'=4,'ribbon_1'=4] {'energy_0'}, dimensions={0} | all-to-all | bytes 1048576 | tf_op jit(solution)/shard_map/all_to_all | solution.py:359
  186.9 2.5 %shard_map.73 = f32[1024,128]{1,0:T(8,128)} custom-call(bf16[256,384]{1,0:T(8,128)(2,1)S(1)} %copy-done.3, bf16[128,384]{1,0:T(8,128)(2,1)S(1)} %copy-done.4, f32[1024,128]{1,0:T(8,128)S(1)} %bitcast.21), custom_call_target="tpu_custom_call" | custom-call | flops 1207959552 | bytes 4194304 | tf_op jit(solution)/shard_map/pallas_call | solution.py:70
  189.4 3.9 %all-to-all-start.1 = ((f32[32,32,128]{2,1,0:T(8,128)}), f32[32,32,128]{2,1,0:T(8,128)S(1)}, u32[]{:S(2)}, u32[]{:S(2)}) async-start(f32[32,32,128]{2,1,0:T(8,128)} %bitcast.10), calls=%async_computation.1 | async-start | bytes 1048576 | tf_op jit(solution)/shard_map/all_to_all | solution.py:366
  193.3 44.3 %all-to-all-done.1 = f32[32,32,128]{2,1,0:T(8,128)S(1)} async-done(((f32[32,32,128]{2,1,0:T(8,128)}), f32[32,32,128]{2,1,0:T(8,128)S(1)}, u32[]{:S(2)}, u32[]{:S(2)}) %all-to-all-start.1) | async-done | bytes 524320 | tf_op jit(solution)/shard_map/all_to_all | solution.py:366
  237.6 1.9 collective-permute-start.12
  239.5 1.5 collective-permute-done.12.theirs
  241.0 1.6 shard_map.74
  (19 shorter events, 1.3 us)
Async XLA Ops:
  0.6 34.5 %copy-start.1 = (f32[1,1,2,256,256]{4,3,2,1,0:T(8,128)S(1)}, f32[1,1,2,256,256]{4,3,2,1,0:T(8,128)}, u32[]{:S(2)}) copy-start(f32[1,1,2,256,256]{4,3,2,1,0:T(8,128)} %param.5) | copy-start | bytes 1572868
  0.6 15.0 %collective-permute-start = (f32[2,256,256]{2,1,0:T(8,128)}, f32[2,256,256]{2,1,0:T(8,128)S(1)}, u32[]{:S(2)}, u32[]{:S(2)}) collective-permute-start(f32[2,256,256]{2,1,0:T(8,128)} %bitcast.24), channel_id=1, source_target_pairs={{0,1},{1,2},{2,3},{3,0},{4,5},{5,6},{6,7},{7,4},{8,9},{9,10},{10,1... | collective-permute-start | bytes 1572872 | tf_op jit(solution)/shard_map/ppermute | solution.py:305
  3.6 14.9 %collective-permute-start.2 = (f32[2,256,256]{2,1,0:T(8,128)}, f32[2,256,256]{2,1,0:T(8,128)S(1)}, u32[]{:S(2)}, u32[]{:S(2)}) collective-permute-start(f32[2,256,256]{2,1,0:T(8,128)} %bitcast.25), channel_id=1, source_target_pairs={{0,3},{1,0},{2,1},{3,2},{4,7},{5,4},{6,5},{7,6},{8,11},{9,8},{10,9... | collective-permute-start | bytes 1572872 | tf_op jit(solution)/shard_map/ppermute | solution.py:305
  6.1 20.9 %collective-permute-start.4 = (f32[2,256,256]{2,1,0:T(8,128)}, f32[2,256,256]{2,1,0:T(8,128)S(1)}, u32[]{:S(2)}, u32[]{:S(2)}) collective-permute-start(f32[2,256,256]{2,1,0:T(8,128)} %bitcast.27), channel_id=1, source_target_pairs={{0,1},{1,2},{2,3},{3,0},{4,5},{5,6},{6,7},{7,4},{8,9},{9,10},{10,1... | collective-permute-start | bytes 1572872 | tf_op jit(solution)/shard_map/ppermute | solution.py:305
  8.9 20.9 %collective-permute-start.6 = (f32[2,256,256]{2,1,0:T(8,128)}, f32[2,256,256]{2,1,0:T(8,128)S(1)}, u32[]{:S(2)}, u32[]{:S(2)}) collective-permute-start(f32[2,256,256]{2,1,0:T(8,128)} %bitcast.28), channel_id=1, source_target_pairs={{0,3},{1,0},{2,1},{3,2},{4,7},{5,4},{6,5},{7,6},{8,11},{9,8},{10,9... | collective-permute-start | bytes 1572872 | tf_op jit(solution)/shard_map/ppermute | solution.py:305
  15.7 16.8 %collective-permute-start.1 = (f32[256,256]{1,0:T(8,128)S(1)}, f32[256,256]{1,0:T(8,128)S(1)}, u32[]{:S(2)}, u32[]{:S(2)}) collective-permute-start(f32[256,256]{1,0:T(8,128)S(1)} %slice_bitcast_fusion.3), channel_id=1, source_target_pairs={{0,1},{1,2},{2,3},{3,0},{4,5},{5,6},{6,7},{7,4},{8,9},{9,10},{10,1... | collective-permute-start | bytes 786440 | tf_op jit(solution)/shard_map/ppermute | solution.py:305
  18.6 16.5 %collective-permute-start.3 = (f32[256,256]{1,0:T(8,128)S(1)}, f32[256,256]{1,0:T(8,128)S(1)}, u32[]{:S(2)}, u32[]{:S(2)}) collective-permute-start(f32[256,256]{1,0:T(8,128)S(1)} %slice_bitcast_fusion.2), channel_id=1, source_target_pairs={{0,3},{1,0},{2,1},{3,2},{4,7},{5,4},{6,5},{7,6},{8,11},{9,8},{10,9... | collective-permute-start | bytes 786440 | tf_op jit(solution)/shard_map/ppermute | solution.py:305
  26.9 11.2 %collective-permute-start.5 = (f32[256,256]{1,0:T(8,128)S(1)}, f32[256,256]{1,0:T(8,128)S(1)}, u32[]{:S(2)}, u32[]{:S(2)}) collective-permute-start(f32[256,256]{1,0:T(8,128)S(1)} %slice_bitcast_fusion.1), channel_id=1, source_target_pairs={{0,1},{1,2},{2,3},{3,0},{4,5},{5,6},{6,7},{7,4},{8,9},{9,10},{10,1... | collective-permute-start | bytes 786440 | tf_op jit(solution)/shard_map/ppermute | solution.py:305
  29.8 10.9 %copy-start.2 = (f32[1,1,2,256,256]{4,3,2,1,0:T(8,128)S(1)}, f32[1,1,2,256,256]{4,3,2,1,0:T(8,128)}, u32[]{:S(2)}) copy-start(f32[1,1,2,256,256]{4,3,2,1,0:T(8,128)} %param.6) | copy-start | bytes 1572868
  29.8 10.8 %collective-permute-start.7 = (f32[256,256]{1,0:T(8,128)S(1)}, f32[256,256]{1,0:T(8,128)S(1)}, u32[]{:S(2)}, u32[]{:S(2)}) collective-permute-start(f32[256,256]{1,0:T(8,128)S(1)} %slice_bitcast_fusion), channel_id=1, source_target_pairs={{0,3},{1,0},{2,1},{3,2},{4,7},{5,4},{6,5},{7,6},{8,11},{9,8},{10,9... | collective-permute-start | bytes 786440 | tf_op jit(solution)/shard_map/ppermute | solution.py:305
  44.2 13.5 %collective-permute-start.9 = (f32[2,256,256]{2,1,0:T(8,128)S(1)}, f32[2,256,256]{2,1,0:T(8,128)S(1)}, u32[]{:S(2)}, u32[]{:S(2)}) collective-permute-start(f32[2,256,256]{2,1,0:T(8,128)S(1)} %get-tuple-element.18.tot_add), channel_id=1, source_target_pairs={{0,4},{4,0},{8,12},{1,5},{5,1},{9,13},{2,6},{6,2},{10,14},{3,7},{7... | collective-permute-start | bytes 1572872 | tf_op jit(solution)/shard_map/ppermute | solution.py:340
  45.5 23.5 %collective-permute-start.8 = (f32[2,256,256]{2,1,0:T(8,128)S(1)}, f32[2,256,256]{2,1,0:T(8,128)S(1)}, u32[]{:S(2)}, u32[]{:S(2)}) collective-permute-start(f32[2,256,256]{2,1,0:T(8,128)S(1)} %get-tuple-element.17.tot_map), channel_id=1, source_target_pairs={{4,0},{8,12},{5,1},{9,13},{6,2},{10,14},{7,3},{11,15},{20,16},{24,... | collective-permute-start | bytes 1572872 | tf_op jit(solution)/shard_map/ppermute | solution.py:334
  70.5 13.9 %collective-permute-start.10 = (f32[2,256,256]{2,1,0:T(8,128)S(1)}, f32[2,256,256]{2,1,0:T(8,128)S(1)}, u32[]{:S(2)}, u32[]{:S(2)}) collective-permute-start(f32[2,256,256]{2,1,0:T(8,128)S(1)} %get-tuple-element.19.joint), channel_id=1, source_target_pairs={{4,8},{0,12},{5,9},{1,13},{6,10},{2,14},{7,11},{3,15},{20,24},{16,... | collective-permute-start | bytes 1572872 | tf_op jit(solution)/shard_map/ppermute | solution.py:345
  84.4 102.5 %copy-start.3 = (bf16[256,384]{1,0:T(8,128)(2,1)S(1)}, bf16[256,384]{1,0:T(8,128)(2,1)}, u32[]{:S(2)}) copy-start(bf16[256,384]{1,0:T(8,128)(2,1)} %constant.19.clone.forward) | copy-start | bytes 589828
  84.4 102.5 %copy-start.4 = (bf16[128,384]{1,0:T(8,128)(2,1)S(1)}, bf16[128,384]{1,0:T(8,128)(2,1)}, u32[]{:S(2)}) copy-start(bf16[128,384]{1,0:T(8,128)(2,1)} %constant.20.clone.backward) | copy-start | bytes 294916
  86.2 6.6 %collective-permute-start.11 = (f32[32,2,8,128]{3,2,1,0:T(8,128)S(1)}, f32[32,2,8,128]{3,2,1,0:T(8,128)S(1)}, u32[]{:S(2)}, u32[]{:S(2)}) collective-permute-start(f32[32,2,8,128]{3,2,1,0:T(8,128)S(1)} %get-tuple-element.23), channel_id=1, source_target_pairs={{0,16},{16,0},{1,17},{17,1},{2,18},{18,2},{3,19},{19,3},{4,20},{20... | collective-permute-start | bytes 786440 | tf_op jit(solution)/shard_map/ppermute | solution.py:357
  186.9 54.1 %copy-start = (f32[1,256,256]{2,1,0:T(8,128)S(1)}, f32[1,256,256]{2,1,0:T(8,128)}, u32[]{:S(2)}) copy-start(f32[1,256,256]{2,1,0:T(8,128)} %param.7) | copy-start | bytes 786436
  189.4 48.2 %all-to-all-start.1 = ((f32[32,32,128]{2,1,0:T(8,128)}), f32[32,32,128]{2,1,0:T(8,128)S(1)}, u32[]{:S(2)}, u32[]{:S(2)}) async-start(f32[32,32,128]{2,1,0:T(8,128)} %bitcast.10), calls=%async_computation.1 | async-start | bytes 1048576 | tf_op jit(solution)/shard_map/all_to_all | solution.py:366
  237.6 3.4 %collective-permute-start.12 = (f32[32,2,8,128]{3,2,1,0:T(8,128)S(1)}, f32[32,2,8,128]{3,2,1,0:T(8,128)S(1)}, u32[]{:S(2)}, u32[]{:S(2)}) collective-permute-start(f32[32,2,8,128]{3,2,1,0:T(8,128)S(1)} %dynamic-slice_bitcast_fusion), channel_id=1, source_target_pairs={{0,16},{16,0},{1,17},{17,1},{2,18},{18,2},{3,19},{19,3},{4,20},{20... | collective-permute-start | bytes 786440 | tf_op jit(solution)/shard_map/ppermute | solution.py:369
where the time goes:
time: 243 us
  waiting for transfers between devices  98 us (40%)
  blocking collectives  70.3 us (29%)
  Pallas kernels  36.7 us (15%)
  starting transfers between devices  36.5 us (15%)
    all_to_all x1, blocking collectives, step(): lax.all_to_all(groups.reshape(count, 4 * rows, 128), 'energy_0', 0, 0, ti...  70.3 us
    all_to_all x1, waiting for transfers between devices, step(): lax.all_to_all(lags.reshape(count, 4 * rows, 128), 'energy_0', 0, 0, tile...  44.3 us
    pallas_call x7, Pallas kernels, run(): pl.pallas_call(body, out_shape=outs, in_specs=[VMEM] * len(args), out_spe...  36.7 us
    ppermute x8, starting transfers between devices, shift(): lax.ppermute(value, axis, [(i, (i + step) % length) for i in range(length)])  21.4 us
    ppermute x8, waiting for transfers between devices, shift(): lax.ppermute(value, axis, [(i, (i + step) % length) for i in range(length)])  16.4 us
    ppermute x1, waiting for transfers between devices, step(): passed = lax.ppermute(joint, 'ribbon_0', [(1, 2), (0, 3)])  12.6 us
    ppermute x1, waiting for transfers between devices, step(): got_map = lax.ppermute(tot_map, 'ribbon_0', [(1, 0), (2, 3)])  11.2 us
    ppermute x1, waiting for transfers between devices, step(): got_add = lax.ppermute(tot_add, 'ribbon_0', [(0, 1), (1, 0), (2, 3)])  10.9 us
  transfers between devices with their start and end apart: 14, of which 12 were waited for; matrix products, arithmetic and copies ran while one was open for 0% of the time, Pallas kernels for 1%

commit v1 on v0

--- a/solution.py
+++ b/solution.py
@@ -12,7 +12,8 @@
 
 F32 = jnp.float32
 BF16 = jnp.bfloat16
-STAGGER = 4500
+STAGGER = 4400
+LEAD = 2000
 VMEM = pl.BlockSpec(memory_space=pltpu.VMEM)
 
 
@@ -78,13 +79,10 @@
     )(*args)
 
 
-def row_map(own, prev, opp_re, opp_im, nxt, order, prefix, total, late, *slots):
+def row_map(own, prev, opp, nxt, order, prefix, total, late, *slots):
     x = lax.axis_index("ribbon_1")
-    for r, ref in ((0, own), (1, prev), (3, nxt)):
+    for r, ref in enumerate((own, prev, opp, nxt)):
         order[lax.rem(x + 4 - r, 4)] = ref[...]
-    across = lax.rem(x + 2, 4)
-    order[across, 0] = opp_re[...]
-    order[across, 1] = opp_im[...]
     a0, a1, a2, a3, pair, upper = slots
     for j, slot in ((0, a0), (1, a1), (2, a2), (3, a3)):
         put(slot, order[j, 0], order[j, 1])
@@ -112,13 +110,10 @@
         prefix[...] = total[...]
 
 
-def row_add(order, late, own, prev, opp_re, opp_im, nxt, prefix, total, adds, *slots):
+def row_add(order, late, own, prev, opp, nxt, prefix, total, adds, *slots):
     x = lax.axis_index("ribbon_1")
-    for r, ref in ((0, own), (1, prev), (3, nxt)):
+    for r, ref in enumerate((own, prev, opp, nxt)):
         adds[lax.rem(x + 4 - r, 4)] = ref[...]
-    across = lax.rem(x + 2, 4)
-    adds[across, 0] = opp_re[...]
-    adds[across, 1] = opp_im[...]
     a, b, c, d, mid, mid2 = slots
     put(a, order[1, 0], order[1, 1])
     put(b, adds[0, 0], adds[0, 1])
@@ -222,15 +217,22 @@
             out[:, p] = part.reshape(count, rows, 128)
 
 
+def core_waits(core, steps, idle):
+    @pl.when(lax.axis_index("energy_1") == core)
+    def _():
+        idle[...] = jnp.zeros_like(idle)
+        idle[...] = lax.fori_loop(0, steps, lambda _, v: v * 0.5 + 1.0, idle[...])
+
+
+def hold(idle):
+    core_waits(1, LEAD, idle)
+
+
 def pack(keep, got, groups, idle):
     c = lax.axis_index("energy_1")
     groups[:, c] = keep[...]
     groups[:, 1 - c] = got[...]
-
-    @pl.when(c == 1)
-    def _():
-        idle[...] = keep[0, 0]
-        idle[...] = lax.fori_loop(0, STAGGER, lambda _, v: v * 0.5 + 1.0, idle[...])
+    core_waits(0, STAGGER, idle)
 
 
 def correlate(forward, backward, given, out, terms):
@@ -305,11 +307,6 @@
     return lax.ppermute(value, axis, [(i, (i + step) % length) for i in range(length)])
 
 
-def gather_row(value):
-    prev, nxt = shift(value, "ribbon_1", 1), shift(value, "ribbon_1", -1)
-    return prev, nxt
-
-
 def step(transfer, source, coulomb):
     a, b, bare = transfer[0, 0], source[0, 0], coulomb[0]
     order = a.shape[-1]
@@ -319,23 +316,27 @@
     slot = pltpu.VMEM((4, 2, order, order), BF16)
     product = 18 * order**3
 
-    a_prev, a_next = gather_row(a)
-    b_prev, b_next = gather_row(b)
-    a_opp_re = shift(a_prev[0], "ribbon_1", 1)
-    a_opp_im = shift(a_next[1], "ribbon_1", -1)
-    b_opp_re = shift(b_prev[0], "ribbon_1", 1)
-    b_opp_im = shift(b_next[1], "ribbon_1", -1)
+    pl.pallas_call(
+        hold, out_shape=jax.ShapeDtypeStruct((8, 128), F32), out_specs=VMEM, name="hold",
+        compiler_params=pltpu.CompilerParams(has_side_effects=True),
+    )()
+    a_prev = shift(a, "ribbon_1", 1)
+    b_next = shift(b, "ribbon_1", -1)
+    b_prev = shift(b, "ribbon_1", 1)
+    a_next = shift(a, "ribbon_1", -1)
+    a_opp = shift(a_prev, "ribbon_1", 1)
+    b_opp = shift(b_next, "ribbon_1", -1)
 
     four = jax.ShapeDtypeStruct((4, 2, order, order), F32)
     maps, pre_map, tot_map, late = run(
         row_map, [four, matrix, matrix, matrix], [slot] * 6, 4 * product,
-        a, a_prev, a_opp_re, a_opp_im, a_next,
+        a, a_prev, a_opp, a_next,
     )
     got_map = lax.ppermute(tot_map, "ribbon_0", [(1, 0), (2, 3)])
     pre_add, tot_add = run(
         row_add, [matrix, matrix], [pltpu.VMEM((4, 2, order, order), F32)] + [slot] * 6,
         8 * product,
-        maps, late, b, b_prev, b_opp_re, b_opp_im, b_next,
+        maps, late, b, b_prev, b_opp, b_next,
     )
     got_add = lax.ppermute(tot_add, "ribbon_0", [(0, 1), (1, 0), (2, 3)])
     joint, new_map = run(

time: 243 us -> 255 us (1.049)
  the two profiles are of different devices: /device:TPU:29 before, /device:TPU:25 now
where the time goes in v1:
time: 255 us; the launch traced here: 254 us
  waiting for transfers between devices  99.5 us (39%)
  blocking collectives  71 us (28%)
  starting transfers between devices  59.2 us (23%)
  Pallas kernels  22.8 us (9%)
    all_to_all x1, blocking collectives, step(): lax.all_to_all(groups.reshape(count, 4 * rows, 128), 'energy_0', 0, 0, ti...  71 us
    all_to_all x1, waiting for transfers between devices, step(): lax.all_to_all(lags.reshape(count, 4 * rows, 128), 'energy_0', 0, 0, tile...  43.1 us
    ppermute x1, starting transfers between devices, step(): halves = lax.ppermute(other_lag, 'energy_1', swap)  27.4 us
    ppermute x6, waiting for transfers between devices, shift(): lax.ppermute(value, axis, [(i, (i + step) % length) for i in range(length)])  21.6 us
    ppermute x6, starting transfers between devices, shift(): lax.ppermute(value, axis, [(i, (i + step) % length) for i in range(length)])  18.1 us
    ppermute x1, waiting for transfers between devices, step(): passed = lax.ppermute(joint, 'ribbon_0', [(1, 2), (0, 3)])  12 us
    pallas_call x7, Pallas kernels, run(): pl.pallas_call(body, out_shape=outs, in_specs=[VMEM] * len(args), out_spe...  11.7 us
    ppermute x1, waiting for transfers between devices, step(): got_map = lax.ppermute(tot_map, 'ribbon_0', [(1, 0), (2, 3)])  11.2 us
  transfers between devices with their start and end apart: 12, of which 9 were waited for; matrix products, arithmetic and copies ran while one was open for 0% of the time, Pallas kernels for 5%

profile of v1, /device:TPU:25, one launch (start us, length us, event | category | flops | bytes accessed | tf_op | source)
XLA Modules:
  0.0 254.4 jit_solution(5937692932214853501)
XLA Ops:
  0.6 3.1 %collective-permute-start = (f32[2,256,256]{2,1,0:T(8,128)}, f32[2,256,256]{2,1,0:T(8,128)S(1)}, u32[]{:S(2)}, u32[]{:S(2)}) collective-permute-start(f32[2,256,256]{2,1,0:T(8,128)} %bitcast.16), channel_id=1, source_target_pairs={{0,1},{1,2},{2,3},{3,0},{4,5},{5,6},{6,7},{7,4},{8,9},{9,10},{10,1... | collective-permute-start | bytes 1572872 | tf_op jit(solution)/shard_map/ppermute | solution.py:307
  3.8 3.4 %collective-permute-start.4 = (f32[2,256,256]{2,1,0:T(8,128)}, f32[2,256,256]{2,1,0:T(8,128)S(1)}, u32[]{:S(2)}, u32[]{:S(2)}) collective-permute-start(f32[2,256,256]{2,1,0:T(8,128)} %bitcast.19), channel_id=1, source_target_pairs={{0,3},{1,0},{2,1},{3,2},{4,7},{5,4},{6,5},{7,6},{8,11},{9,8},{10,9... | collective-permute-start | bytes 1572872 | tf_op jit(solution)/shard_map/ppermute | solution.py:307
  7.1 3.2 %collective-permute-start.2 = (f32[2,256,256]{2,1,0:T(8,128)}, f32[2,256,256]{2,1,0:T(8,128)S(1)}, u32[]{:S(2)}, u32[]{:S(2)}) collective-permute-start(f32[2,256,256]{2,1,0:T(8,128)} %bitcast.17), channel_id=1, source_target_pairs={{0,3},{1,0},{2,1},{3,2},{4,7},{5,4},{6,5},{7,6},{8,11},{9,8},{10,9... | collective-permute-start | bytes 1572872 | tf_op jit(solution)/shard_map/ppermute | solution.py:307
  10.3 6.4 %collective-permute-done.prev = f32[2,256,256]{2,1,0:T(8,128)S(1)} collective-permute-done((f32[2,256,256]{2,1,0:T(8,128)}, f32[2,256,256]{2,1,0:T(8,128)S(1)}, u32[]{:S(2)}, u32[]{:S(2)}) %collective-permute-start) | collective-permute-done | bytes 524320 | tf_op jit(solution)/shard_map/ppermute | solution.py:307
  16.8 1.9 collective-permute-start.1
  18.7 3.1 %collective-permute-start.3 = (f32[2,256,256]{2,1,0:T(8,128)}, f32[2,256,256]{2,1,0:T(8,128)S(1)}, u32[]{:S(2)}, u32[]{:S(2)}) collective-permute-start(f32[2,256,256]{2,1,0:T(8,128)} %bitcast.20), channel_id=1, source_target_pairs={{0,1},{1,2},{2,3},{3,0},{4,5},{5,6},{6,7},{7,4},{8,9},{9,10},{10,1... | collective-permute-start | bytes 1572872 | tf_op jit(solution)/shard_map/ppermute | solution.py:307
  21.8 0.0 collective-permute-done.4.nxt
  21.8 3.4 %collective-permute-start.5 = (f32[2,256,256]{2,1,0:T(8,128)S(1)}, f32[2,256,256]{2,1,0:T(8,128)S(1)}, u32[]{:S(2)}, u32[]{:S(2)}) collective-permute-start(f32[2,256,256]{2,1,0:T(8,128)S(1)} %collective-permute-done.4.nxt), channel_id=1, source_target_pairs={{0,3},{1,0},{2,1},{3,2},{4,7},{5,4},{6,5},{7,6},{8,11},{9,8},{10,9... | collective-permute-start | bytes 1572872 | tf_op jit(solution)/shard_map/ppermute | solution.py:307
  25.2 4.4 %collective-permute-done.2.nxt = f32[2,256,256]{2,1,0:T(8,128)S(1)} collective-permute-done((f32[2,256,256]{2,1,0:T(8,128)}, f32[2,256,256]{2,1,0:T(8,128)S(1)}, u32[]{:S(2)}, u32[]{:S(2)}) %collective-permute-start.2) | collective-permute-done | bytes 524320 | tf_op jit(solution)/shard_map/ppermute | solution.py:307
  29.6 2.2 collective-permute-done.1.opp
  31.8 1.0 copy-done.1
  32.8 1.6 shard_map.68
  34.4 8.6 %collective-permute-done.3.prev = f32[2,256,256]{2,1,0:T(8,128)S(1)} collective-permute-done((f32[2,256,256]{2,1,0:T(8,128)}, f32[2,256,256]{2,1,0:T(8,128)S(1)}, u32[]{:S(2)}, u32[]{:S(2)}) %collective-permute-start.3) | collective-permute-done | bytes 524320 | tf_op jit(solution)/shard_map/ppermute | solution.py:307
  43.0 0.0 collective-permute-done.5.opp
  43.0 2.7 %shard_map.69 = (f32[2,256,256]{2,1,0:T(8,128)S(1)}, f32[2,256,256]{2,1,0:T(8,128)S(1)}) custom-call(f32[4,2,256,256]{3,2,1,0:T(8,128)S(1)} %get-tuple-element.13.order, f32[2,256,256]{2,1,0:T(8,128)S(1)} %get-tuple-element.14.late, f32[2,256,256]{2,1,0:T(8,128)S(1)} %bitcast.21, f32[2,256,256]{2,1,0:T(8,128)S(1)} %collective-permute-done.3.prev, ...), custom_call_target="tpu_custom_call" | custom-call | flops 2415919104 | bytes 4194304 | tf_op jit(solution)/shard_map/pallas_call | solution.py:71
  45.7 1.3 collective-permute-start.7
  47.0 1.3 collective-permute-start.6
  48.3 10.4 %collective-permute-done.7.got_add = f32[2,256,256]{2,1,0:T(8,128)S(1)} collective-permute-done((f32[2,256,256]{2,1,0:T(8,128)S(1)}, f32[2,256,256]{2,1,0:T(8,128)S(1)}, u32[]{:S(2)}, u32[]{:S(2)}) %collective-permute-start.7) | collective-permute-done | bytes 524320 | tf_op jit(solution)/shard_map/ppermute | solution.py:341
  58.7 11.2 %collective-permute-done.6.got_map = f32[2,256,256]{2,1,0:T(8,128)S(1)} collective-permute-done((f32[2,256,256]{2,1,0:T(8,128)S(1)}, f32[2,256,256]{2,1,0:T(8,128)S(1)}, u32[]{:S(2)}, u32[]{:S(2)}) %collective-permute-start.6) | collective-permute-done | bytes 524320 | tf_op jit(solution)/shard_map/ppermute | solution.py:335
  69.9 1.5 shard_map.70
  71.5 1.3 collective-permute-start.8
  72.8 12.0 %collective-permute-done.8.passed = f32[2,256,256]{2,1,0:T(8,128)S(1)} collective-permute-done((f32[2,256,256]{2,1,0:T(8,128)S(1)}, f32[2,256,256]{2,1,0:T(8,128)S(1)}, u32[]{:S(2)}, u32[]{:S(2)}) %collective-permute-start.8) | collective-permute-done | bytes 524320 | tf_op jit(solution)/shard_map/ppermute | solution.py:346
  84.8 1.8 shard_map.71
  86.6 6.0 %collective-permute-start.9 = (f32[32,2,8,128]{3,2,1,0:T(8,128)S(1)}, f32[32,2,8,128]{3,2,1,0:T(8,128)S(1)}, u32[]{:S(2)}, u32[]{:S(2)}) collective-permute-start(f32[32,2,8,128]{3,2,1,0:T(8,128)S(1)} %get-tuple-element.23), channel_id=1, source_target_pairs={{0,16},{16,0},{1,17},{17,1},{2,18},{18,2},{3,19},{19,3},{4,20},{20... | collective-permute-start | bytes 786440 | tf_op jit(solution)/shard_map/ppermute | solution.py:358
  92.6 1.1 collective-permute-done.9.got
  93.8 71.0 %all_to_all.10 = f32[32,32,128]{2,1,0:T(8,128)S(1)} all-to-all(f32[32,32,128]{2,1,0:T(8,128)S(1)} %bitcast.14), channel_id=1, replica_groups=mesh['energy_0'=32,'energy_1'=2,'ribbon_0'=4,'ribbon_1'=4] {'energy_0'}, dimensions={0} | all-to-all | bytes 1048576 | tf_op jit(solution)/shard_map/all_to_all | solution.py:360
  164.8 2.5 shard_map.73
  167.3 3.9 %all-to-all-start.1 = ((f32[32,32,128]{2,1,0:T(8,128)}), f32[32,32,128]{2,1,0:T(8,128)S(1)}, u32[]{:S(2)}, u32[]{:S(2)}) async-start(f32[32,32,128]{2,1,0:T(8,128)} %bitcast.6), calls=%async_computation.1 | async-start | bytes 1048576 | tf_op jit(solution)/shard_map/all_to_all | solution.py:367
  171.2 43.1 %all-to-all-done.1 = f32[32,32,128]{2,1,0:T(8,128)S(1)} async-done(((f32[32,32,128]{2,1,0:T(8,128)}), f32[32,32,128]{2,1,0:T(8,128)S(1)}, u32[]{:S(2)}, u32[]{:S(2)}) %all-to-all-start.1) | async-done | bytes 524320 | tf_op jit(solution)/shard_map/all_to_all | solution.py:367
  214.3 27.4 %collective-permute-start.10 = (f32[32,2,8,128]{3,2,1,0:T(8,128)S(1)}, f32[32,2,8,128]{3,2,1,0:T(8,128)S(1)}, u32[]{:S(2)}, u32[]{:S(2)}) collective-permute-start(f32[32,2,8,128]{3,2,1,0:T(8,128)S(1)} %dynamic-slice_bitcast_fusion), channel_id=1, source_target_pairs={{0,16},{16,0},{1,17},{17,1},{2,18},{18,2},{3,19},{19,3},{4,20},{20... | collective-permute-start | bytes 786440 | tf_op jit(solution)/shard_map/ppermute | solution.py:370
  241.7 11.1 %hold.1 = f32[8,128]{1,0:T(8,128)} custom-call(), custom_call_target="tpu_custom_call" | custom-call | tf_op jit(solution)/shard_map/hold/pallas_call | solution.py:319
  252.8 1.6 shard_map.74
  (12 shorter events, 0.1 us)
Async XLA Ops:
  0.6 16.1 %collective-permute-start = (f32[2,256,256]{2,1,0:T(8,128)}, f32[2,256,256]{2,1,0:T(8,128)S(1)}, u32[]{:S(2)}, u32[]{:S(2)}) collective-permute-start(f32[2,256,256]{2,1,0:T(8,128)} %bitcast.16), channel_id=1, source_target_pairs={{0,1},{1,2},{2,3},{3,0},{4,5},{5,6},{6,7},{7,4},{8,9},{9,10},{10,1... | collective-permute-start | bytes 1572872 | tf_op jit(solution)/shard_map/ppermute | solution.py:307
  3.8 18.0 %collective-permute-start.4 = (f32[2,256,256]{2,1,0:T(8,128)}, f32[2,256,256]{2,1,0:T(8,128)S(1)}, u32[]{:S(2)}, u32[]{:S(2)}) collective-permute-start(f32[2,256,256]{2,1,0:T(8,128)} %bitcast.19), channel_id=1, source_target_pairs={{0,3},{1,0},{2,1},{3,2},{4,7},{5,4},{6,5},{7,6},{8,11},{9,8},{10,9... | collective-permute-start | bytes 1572872 | tf_op jit(solution)/shard_map/ppermute | solution.py:307
  7.1 22.5 %collective-permute-start.2 = (f32[2,256,256]{2,1,0:T(8,128)}, f32[2,256,256]{2,1,0:T(8,128)S(1)}, u32[]{:S(2)}, u32[]{:S(2)}) collective-permute-start(f32[2,256,256]{2,1,0:T(8,128)} %bitcast.17), channel_id=1, source_target_pairs={{0,3},{1,0},{2,1},{3,2},{4,7},{5,4},{6,5},{7,6},{8,11},{9,8},{10,9... | collective-permute-start | bytes 1572872 | tf_op jit(solution)/shard_map/ppermute | solution.py:307
  16.8 15.0 %collective-permute-start.1 = (f32[2,256,256]{2,1,0:T(8,128)S(1)}, f32[2,256,256]{2,1,0:T(8,128)S(1)}, u32[]{:S(2)}, u32[]{:S(2)}) collective-permute-start(f32[2,256,256]{2,1,0:T(8,128)S(1)} %collective-permute-done.prev), channel_id=1, source_target_pairs={{0,1},{1,2},{2,3},{3,0},{4,5},{5,6},{6,7},{7,4},{8,9},{9,10},{10,1... | collective-permute-start | bytes 1572872 | tf_op jit(solution)/shard_map/ppermute | solution.py:307
  18.7 24.4 %collective-permute-start.3 = (f32[2,256,256]{2,1,0:T(8,128)}, f32[2,256,256]{2,1,0:T(8,128)S(1)}, u32[]{:S(2)}, u32[]{:S(2)}) collective-permute-start(f32[2,256,256]{2,1,0:T(8,128)} %bitcast.20), channel_id=1, source_target_pairs={{0,1},{1,2},{2,3},{3,0},{4,5},{5,6},{6,7},{7,4},{8,9},{9,10},{10,1... | collective-permute-start | bytes 1572872 | tf_op jit(solution)/shard_map/ppermute | solution.py:307
  21.8 21.2 %collective-permute-start.5 = (f32[2,256,256]{2,1,0:T(8,128)S(1)}, f32[2,256,256]{2,1,0:T(8,128)S(1)}, u32[]{:S(2)}, u32[]{:S(2)}) collective-permute-start(f32[2,256,256]{2,1,0:T(8,128)S(1)} %collective-permute-done.4.nxt), channel_id=1, source_target_pairs={{0,3},{1,0},{2,1},{3,2},{4,7},{5,4},{6,5},{7,6},{8,11},{9,8},{10,9... | collective-permute-start | bytes 1572872 | tf_op jit(solution)/shard_map/ppermute | solution.py:307
  31.8 1.0 copy-start.1
  32.8 10.2 %copy-start.2 = (f32[1,1,2,256,256]{4,3,2,1,0:T(8,128)S(1)}, f32[1,1,2,256,256]{4,3,2,1,0:T(8,128)}, u32[]{:S(2)}) copy-start(f32[1,1,2,256,256]{4,3,2,1,0:T(8,128)} %param.6) | copy-start | bytes 1572868
  45.7 13.0 %collective-permute-start.7 = (f32[2,256,256]{2,1,0:T(8,128)S(1)}, f32[2,256,256]{2,1,0:T(8,128)S(1)}, u32[]{:S(2)}, u32[]{:S(2)}) collective-permute-start(f32[2,256,256]{2,1,0:T(8,128)S(1)} %get-tuple-element.18.tot_add), channel_id=1, source_target_pairs={{0,4},{4,0},{8,12},{1,5},{5,1},{9,13},{2,6},{6,2},{10,14},{3,7},{7... | collective-permute-start | bytes 1572872 | tf_op jit(solution)/shard_map/ppermute | solution.py:341
  47.0 22.9 %collective-permute-start.6 = (f32[2,256,256]{2,1,0:T(8,128)S(1)}, f32[2,256,256]{2,1,0:T(8,128)S(1)}, u32[]{:S(2)}, u32[]{:S(2)}) collective-permute-start(f32[2,256,256]{2,1,0:T(8,128)S(1)} %get-tuple-element.17.tot_map), channel_id=1, source_target_pairs={{4,0},{8,12},{5,1},{9,13},{6,2},{10,14},{7,3},{11,15},{20,16},{24,... | collective-permute-start | bytes 1572872 | tf_op jit(solution)/shard_map/ppermute | solution.py:335
  71.5 13.3 %collective-permute-start.8 = (f32[2,256,256]{2,1,0:T(8,128)S(1)}, f32[2,256,256]{2,1,0:T(8,128)S(1)}, u32[]{:S(2)}, u32[]{:S(2)}) collective-permute-start(f32[2,256,256]{2,1,0:T(8,128)S(1)} %get-tuple-element.19.joint), channel_id=1, source_target_pairs={{4,8},{0,12},{5,9},{1,13},{6,10},{2,14},{7,11},{3,15},{20,24},{16,... | collective-permute-start | bytes 1572872 | tf_op jit(solution)/shard_map/ppermute | solution.py:346
  84.8 80.0 %copy-start.3 = (bf16[256,384]{1,0:T(8,128)(2,1)S(1)}, bf16[256,384]{1,0:T(8,128)(2,1)}, u32[]{:S(2)}) copy-start(bf16[256,384]{1,0:T(8,128)(2,1)} %constant.19.clone.forward) | copy-start | bytes 589828
  84.8 80.0 %copy-start.4 = (bf16[128,384]{1,0:T(8,128)(2,1)S(1)}, bf16[128,384]{1,0:T(8,128)(2,1)}, u32[]{:S(2)}) copy-start(bf16[128,384]{1,0:T(8,128)(2,1)} %constant.20.clone.backward) | copy-start | bytes 294916
  86.6 7.1 %collective-permute-start.9 = (f32[32,2,8,128]{3,2,1,0:T(8,128)S(1)}, f32[32,2,8,128]{3,2,1,0:T(8,128)S(1)}, u32[]{:S(2)}, u32[]{:S(2)}) collective-permute-start(f32[32,2,8,128]{3,2,1,0:T(8,128)S(1)} %get-tuple-element.23), channel_id=1, source_target_pairs={{0,16},{16,0},{1,17},{17,1},{2,18},{18,2},{3,19},{19,3},{4,20},{20... | collective-permute-start | bytes 786440 | tf_op jit(solution)/shard_map/ppermute | solution.py:358
  164.8 88.0 %copy-start = (f32[1,256,256]{2,1,0:T(8,128)S(1)}, f32[1,256,256]{2,1,0:T(8,128)}, u32[]{:S(2)}) copy-start(f32[1,256,256]{2,1,0:T(8,128)} %param.7) | copy-start | bytes 786436
  167.3 47.0 %all-to-all-start.1 = ((f32[32,32,128]{2,1,0:T(8,128)}), f32[32,32,128]{2,1,0:T(8,128)S(1)}, u32[]{:S(2)}, u32[]{:S(2)}) async-start(f32[32,32,128]{2,1,0:T(8,128)} %bitcast.6), calls=%async_computation.1 | async-start | bytes 1048576 | tf_op jit(solution)/shard_map/all_to_all | solution.py:367
  214.3 38.5 %collective-permute-start.10 = (f32[32,2,8,128]{3,2,1,0:T(8,128)S(1)}, f32[32,2,8,128]{3,2,1,0:T(8,128)S(1)}, u32[]{:S(2)}, u32[]{:S(2)}) collective-permute-start(f32[32,2,8,128]{3,2,1,0:T(8,128)S(1)} %dynamic-slice_bitcast_fusion), channel_id=1, source_target_pairs={{0,16},{16,0},{1,17},{17,1},{2,18},{18,2},{3,19},{19,3},{4,20},{20... | collective-permute-start | bytes 786440 | tf_op jit(solution)/shard_map/ppermute | solution.py:370

commit v2 on v1

--- a/solution.py
+++ b/solution.py
@@ -12,8 +12,8 @@
 
 F32 = jnp.float32
 BF16 = jnp.bfloat16
-STAGGER = 4400
-LEAD = 2000
+STAGGER = 4200
+LEAD = 2500
 VMEM = pl.BlockSpec(memory_space=pltpu.VMEM)
 
 
@@ -261,22 +261,32 @@
                 ]
 
 
-def screen(bare, mine, theirs, out, both):
+def bare_times(bare, parts):
+    high, low = split(bare)
+    wide = jnp.concatenate([high, high, low], axis=1)
+    high, low = split(jnp.concatenate(parts, axis=1))
+    half = dot(wide, jnp.concatenate([high, low, high], axis=0))
+    return half[:, :128], half[:, 128:]
+
+
+def screen_own(bare, mine, out):
     c = lax.axis_index("energy_1")
     order = bare.shape[0]
+    parts = [mine[:, c, p].reshape(order, 128) for p in range(2)]
+    out[0], out[1] = bare_times(bare[...], parts)
+
+
+def screen(bare, own, theirs, out, both):
+    c = lax.axis_index("energy_1")
+    order = bare.shape[0]
+    both[c] = own[...]
+    parts = [theirs[:, p].reshape(order, 128) for p in range(2)]
+    both[1 - c, 0], both[1 - c, 1] = bare_times(bare[...], parts)
     high, low = split(bare[...])
-    wide = jnp.concatenate([high, high, low], axis=1)
-    wide_t = jnp.concatenate([high, low, high], axis=1)
-    own = [mine[:, c, p].reshape(order, 128) for p in range(2)]
-    other = [theirs[:, p].reshape(order, 128) for p in range(2)]
-    for at, parts in ((c, own), (1 - c, other)):
-        high, low = split(jnp.concatenate(parts, axis=1))
-        half = dot(wide, jnp.concatenate([high, low, high], axis=0))
-        both[at, 0] = half[:, :128]
-        both[at, 1] = half[:, 128:]
+    wide = jnp.concatenate([high, low, high], axis=1)
     for p in range(2):
         high, low = split(jnp.concatenate([both[0, p], both[1, p]], axis=1))
-        full = dot_t(jnp.concatenate([high, high, low], axis=1), wide_t) * (1.0 / order)
+        full = dot_t(jnp.concatenate([high, high, low], axis=1), wide) * (1.0 / order)
         out[p] = bare[...] + full if p == 0 else full
 
 
@@ -368,9 +378,13 @@
     returned = returned.reshape(count, 2, 2, rows, 128)
     other_lag = lax.dynamic_index_in_dim(returned, 1 - c, 1, keepdims=False)
     halves = lax.ppermute(other_lag, "energy_1", swap)
+    own_part = run(
+        screen_own, jax.ShapeDtypeStruct((2, order, 128), F32), [], product,
+        bare, returned,
+    )
     screened = run(
         screen, matrix, [pltpu.VMEM((2, 2, order, 128), F32)], product,
-        bare, returned, halves,
+        bare, own_part, halves,
     )
     return (lesser[None, None], screened[None, None])
 

time: 255 us -> 257 us (level)
  Pallas kernels: 22.8 us -> 25.7 us
    pallas_call x1, Pallas kernels: 11.1 us -> 13.8 us  [step(): pl.pallas_call(hold, out_shape=jax.ShapeDtypeStruct((8, 128), F32), out_s...]
    pallas_call x7 -> x8, Pallas kernels: 11.7 us -> 11.9 us  [run(): pl.pallas_call(body, out_shape=outs, in_specs=[VMEM] * len(args), out_spe...]
  transfers between devices with their start and end apart: 12 -> 12, of which waited for: 9 -> 9; matrix products, arithmetic and copies ran while one was open for 0% -> 0% of each run, Pallas kernels for 5% -> 6%
where the time goes in v2:
time: 257 us; the launch traced here: 256 us
  waiting for transfers between devices  99.5 us (39%)
  blocking collectives  71 us (28%)
  starting transfers between devices  58 us (23%)
  Pallas kernels  25.7 us (10%)
    all_to_all x1, blocking collectives, step(): lax.all_to_all(groups.reshape(count, 4 * rows, 128), 'energy_0', 0, 0, ti...  71 us
    all_to_all x1, waiting for transfers between devices, step(): lax.all_to_all(lags.reshape(count, 4 * rows, 128), 'energy_0', 0, 0, tile...  43.1 us
    ppermute x1, starting transfers between devices, step(): halves = lax.ppermute(other_lag, 'energy_1', swap)  26.1 us
    ppermute x6, waiting for transfers between devices, shift(): lax.ppermute(value, axis, [(i, (i + step) % length) for i in range(length)])  21.6 us
    ppermute x6, starting transfers between devices, shift(): lax.ppermute(value, axis, [(i, (i + step) % length) for i in range(length)])  18.1 us
    pallas_call x1, Pallas kernels, step(): pl.pallas_call(hold, out_shape=jax.ShapeDtypeStruct((8, 128), F32), out_s...  13.8 us
    ppermute x1, waiting for transfers between devices, step(): passed = lax.ppermute(joint, 'ribbon_0', [(1, 2), (0, 3)])  12 us
    pallas_call x8, Pallas kernels, run(): pl.pallas_call(body, out_shape=outs, in_specs=[VMEM] * len(args), out_spe...  11.9 us
  transfers between devices with their start and end apart: 12, of which 9 were waited for; matrix products, arithmetic and copies ran while one was open for 0% of the time, Pallas kernels for 6%

profile of v2, /device:TPU:25, one launch (start us, length us, event | category | flops | bytes accessed | tf_op | source)
XLA Modules:
  0.0 256.0 jit_solution(18135153741892938314)
XLA Ops:
  0.6 3.1 %collective-permute-start = (f32[2,256,256]{2,1,0:T(8,128)}, f32[2,256,256]{2,1,0:T(8,128)S(1)}, u32[]{:S(2)}, u32[]{:S(2)}) collective-permute-start(f32[2,256,256]{2,1,0:T(8,128)} %bitcast.17), channel_id=1, source_target_pairs={{0,1},{1,2},{2,3},{3,0},{4,5},{5,6},{6,7},{7,4},{8,9},{9,10},{10,1... | collective-permute-start | bytes 1572872 | tf_op jit(solution)/shard_map/ppermute | solution.py:317
  3.8 3.4 %collective-permute-start.4 = (f32[2,256,256]{2,1,0:T(8,128)}, f32[2,256,256]{2,1,0:T(8,128)S(1)}, u32[]{:S(2)}, u32[]{:S(2)}) collective-permute-start(f32[2,256,256]{2,1,0:T(8,128)} %bitcast.20), channel_id=1, source_target_pairs={{0,3},{1,0},{2,1},{3,2},{4,7},{5,4},{6,5},{7,6},{8,11},{9,8},{10,9... | collective-permute-start | bytes 1572872 | tf_op jit(solution)/shard_map/ppermute | solution.py:317
  7.1 3.2 %collective-permute-start.2 = (f32[2,256,256]{2,1,0:T(8,128)}, f32[2,256,256]{2,1,0:T(8,128)S(1)}, u32[]{:S(2)}, u32[]{:S(2)}) collective-permute-start(f32[2,256,256]{2,1,0:T(8,128)} %bitcast.18), channel_id=1, source_target_pairs={{0,3},{1,0},{2,1},{3,2},{4,7},{5,4},{6,5},{7,6},{8,11},{9,8},{10,9... | collective-permute-start | bytes 1572872 | tf_op jit(solution)/shard_map/ppermute | solution.py:317
  10.3 6.4 %collective-permute-done.prev = f32[2,256,256]{2,1,0:T(8,128)S(1)} collective-permute-done((f32[2,256,256]{2,1,0:T(8,128)}, f32[2,256,256]{2,1,0:T(8,128)S(1)}, u32[]{:S(2)}, u32[]{:S(2)}) %collective-permute-start) | collective-permute-done | bytes 524320 | tf_op jit(solution)/shard_map/ppermute | solution.py:317
  16.8 1.9 collective-permute-start.1
  18.7 3.1 %collective-permute-start.3 = (f32[2,256,256]{2,1,0:T(8,128)}, f32[2,256,256]{2,1,0:T(8,128)S(1)}, u32[]{:S(2)}, u32[]{:S(2)}) collective-permute-start(f32[2,256,256]{2,1,0:T(8,128)} %bitcast.21), channel_id=1, source_target_pairs={{0,1},{1,2},{2,3},{3,0},{4,5},{5,6},{6,7},{7,4},{8,9},{9,10},{10,1... | collective-permute-start | bytes 1572872 | tf_op jit(solution)/shard_map/ppermute | solution.py:317
  21.8 0.0 collective-permute-done.4.nxt
  21.8 3.4 %collective-permute-start.5 = (f32[2,256,256]{2,1,0:T(8,128)S(1)}, f32[2,256,256]{2,1,0:T(8,128)S(1)}, u32[]{:S(2)}, u32[]{:S(2)}) collective-permute-start(f32[2,256,256]{2,1,0:T(8,128)S(1)} %collective-permute-done.4.nxt), channel_id=1, source_target_pairs={{0,3},{1,0},{2,1},{3,2},{4,7},{5,4},{6,5},{7,6},{8,11},{9,8},{10,9... | collective-permute-start | bytes 1572872 | tf_op jit(solution)/shard_map/ppermute | solution.py:317
  25.2 4.4 %collective-permute-done.2.nxt = f32[2,256,256]{2,1,0:T(8,128)S(1)} collective-permute-done((f32[2,256,256]{2,1,0:T(8,128)}, f32[2,256,256]{2,1,0:T(8,128)S(1)}, u32[]{:S(2)}, u32[]{:S(2)}) %collective-permute-start.2) | collective-permute-done | bytes 524320 | tf_op jit(solution)/shard_map/ppermute | solution.py:317
  29.6 2.2 collective-permute-done.1.opp
  31.8 1.0 copy-done.1
  32.8 1.6 shard_map.68
  34.4 8.6 %collective-permute-done.3.prev = f32[2,256,256]{2,1,0:T(8,128)S(1)} collective-permute-done((f32[2,256,256]{2,1,0:T(8,128)}, f32[2,256,256]{2,1,0:T(8,128)S(1)}, u32[]{:S(2)}, u32[]{:S(2)}) %collective-permute-start.3) | collective-permute-done | bytes 524320 | tf_op jit(solution)/shard_map/ppermute | solution.py:317
  43.0 2.7 %shard_map.69 = (f32[2,256,256]{2,1,0:T(8,128)S(1)}, f32[2,256,256]{2,1,0:T(8,128)S(1)}) custom-call(f32[4,2,256,256]{3,2,1,0:T(8,128)S(1)} %get-tuple-element.13.order, f32[2,256,256]{2,1,0:T(8,128)S(1)} %get-tuple-element.14.late, f32[2,256,256]{2,1,0:T(8,128)S(1)} %bitcast.22, f32[2,256,256]{2,1,0:T(8,128)S(1)} %collective-permute-done.3.prev, ...), custom_call_target="tpu_custom_call" | custom-call | flops 2415919104 | bytes 4194304 | tf_op jit(solution)/shard_map/pallas_call | solution.py:71
  45.7 1.3 collective-permute-start.7
  47.0 1.3 collective-permute-start.6
  48.3 10.4 %collective-permute-done.7.got_add = f32[2,256,256]{2,1,0:T(8,128)S(1)} collective-permute-done((f32[2,256,256]{2,1,0:T(8,128)S(1)}, f32[2,256,256]{2,1,0:T(8,128)S(1)}, u32[]{:S(2)}, u32[]{:S(2)}) %collective-permute-start.7) | collective-permute-done | bytes 524320 | tf_op jit(solution)/shard_map/ppermute | solution.py:351
  58.7 11.2 %collective-permute-done.6.got_map = f32[2,256,256]{2,1,0:T(8,128)S(1)} collective-permute-done((f32[2,256,256]{2,1,0:T(8,128)S(1)}, f32[2,256,256]{2,1,0:T(8,128)S(1)}, u32[]{:S(2)}, u32[]{:S(2)}) %collective-permute-start.6) | collective-permute-done | bytes 524320 | tf_op jit(solution)/shard_map/ppermute | solution.py:345
  69.9 1.5 shard_map.70
  71.5 1.3 collective-permute-start.8
  72.8 12.0 %collective-permute-done.8.passed = f32[2,256,256]{2,1,0:T(8,128)S(1)} collective-permute-done((f32[2,256,256]{2,1,0:T(8,128)S(1)}, f32[2,256,256]{2,1,0:T(8,128)S(1)}, u32[]{:S(2)}, u32[]{:S(2)}) %collective-permute-start.8) | collective-permute-done | bytes 524320 | tf_op jit(solution)/shard_map/ppermute | solution.py:356
  84.8 1.8 shard_map.71
  86.6 6.0 %collective-permute-start.9 = (f32[32,2,8,128]{3,2,1,0:T(8,128)S(1)}, f32[32,2,8,128]{3,2,1,0:T(8,128)S(1)}, u32[]{:S(2)}, u32[]{:S(2)}) collective-permute-start(f32[32,2,8,128]{3,2,1,0:T(8,128)S(1)} %get-tuple-element.23), channel_id=1, source_target_pairs={{0,16},{16,0},{1,17},{17,1},{2,18},{18,2},{3,19},{19,3},{4,20},{20... | collective-permute-start | bytes 786440 | tf_op jit(solution)/shard_map/ppermute | solution.py:368
  92.6 1.1 collective-permute-done.9.got
  93.8 71.0 %all_to_all.10 = f32[32,32,128]{2,1,0:T(8,128)S(1)} all-to-all(f32[32,32,128]{2,1,0:T(8,128)S(1)} %bitcast.14), channel_id=1, replica_groups=mesh['energy_0'=32,'energy_1'=2,'ribbon_0'=4,'ribbon_1'=4] {'energy_0'}, dimensions={0} | all-to-all | bytes 1048576 | tf_op jit(solution)/shard_map/all_to_all | solution.py:370
  164.8 2.5 shard_map.73
  167.3 3.9 %all-to-all-start.1 = ((f32[32,32,128]{2,1,0:T(8,128)}), f32[32,32,128]{2,1,0:T(8,128)S(1)}, u32[]{:S(2)}, u32[]{:S(2)}) async-start(f32[32,32,128]{2,1,0:T(8,128)} %bitcast.6), calls=%async_computation.1 | async-start | bytes 1048576 | tf_op jit(solution)/shard_map/all_to_all | solution.py:377
  171.2 43.1 %all-to-all-done.1 = f32[32,32,128]{2,1,0:T(8,128)S(1)} async-done(((f32[32,32,128]{2,1,0:T(8,128)}), f32[32,32,128]{2,1,0:T(8,128)S(1)}, u32[]{:S(2)}, u32[]{:S(2)}) %all-to-all-start.1) | async-done | bytes 524320 | tf_op jit(solution)/shard_map/all_to_all | solution.py:377
  214.3 26.1 %collective-permute-start.10 = (f32[32,2,8,128]{3,2,1,0:T(8,128)S(1)}, f32[32,2,8,128]{3,2,1,0:T(8,128)S(1)}, u32[]{:S(2)}, u32[]{:S(2)}) collective-permute-start(f32[32,2,8,128]{3,2,1,0:T(8,128)S(1)} %dynamic-slice_bitcast_fusion), channel_id=1, source_target_pairs={{0,16},{16,0},{1,17},{17,1},{2,18},{18,2},{3,19},{19,3},{4,20},{20... | collective-permute-start | bytes 786440 | tf_op jit(solution)/shard_map/ppermute | solution.py:380
  240.5 13.8 %hold.1 = f32[8,128]{1,0:T(8,128)} custom-call(), custom_call_target="tpu_custom_call" | custom-call | tf_op jit(solution)/shard_map/hold/pallas_call | solution.py:329
  254.2 0.3 shard_map.74.own
  254.5 1.5 shard_map.75
  (13 shorter events, 0.1 us)
Async XLA Ops:
  0.6 16.1 %collective-permute-start = (f32[2,256,256]{2,1,0:T(8,128)}, f32[2,256,256]{2,1,0:T(8,128)S(1)}, u32[]{:S(2)}, u32[]{:S(2)}) collective-permute-start(f32[2,256,256]{2,1,0:T(8,128)} %bitcast.17), channel_id=1, source_target_pairs={{0,1},{1,2},{2,3},{3,0},{4,5},{5,6},{6,7},{7,4},{8,9},{9,10},{10,1... | collective-permute-start | bytes 1572872 | tf_op jit(solution)/shard_map/ppermute | solution.py:317
  3.8 18.0 %collective-permute-start.4 = (f32[2,256,256]{2,1,0:T(8,128)}, f32[2,256,256]{2,1,0:T(8,128)S(1)}, u32[]{:S(2)}, u32[]{:S(2)}) collective-permute-start(f32[2,256,256]{2,1,0:T(8,128)} %bitcast.20), channel_id=1, source_target_pairs={{0,3},{1,0},{2,1},{3,2},{4,7},{5,4},{6,5},{7,6},{8,11},{9,8},{10,9... | collective-permute-start | bytes 1572872 | tf_op jit(solution)/shard_map/ppermute | solution.py:317
  7.1 22.5 %collective-permute-start.2 = (f32[2,256,256]{2,1,0:T(8,128)}, f32[2,256,256]{2,1,0:T(8,128)S(1)}, u32[]{:S(2)}, u32[]{:S(2)}) collective-permute-start(f32[2,256,256]{2,1,0:T(8,128)} %bitcast.18), channel_id=1, source_target_pairs={{0,3},{1,0},{2,1},{3,2},{4,7},{5,4},{6,5},{7,6},{8,11},{9,8},{10,9... | collective-permute-start | bytes 1572872 | tf_op jit(solution)/shard_map/ppermute | solution.py:317
  16.8 15.0 %collective-permute-start.1 = (f32[2,256,256]{2,1,0:T(8,128)S(1)}, f32[2,256,256]{2,1,0:T(8,128)S(1)}, u32[]{:S(2)}, u32[]{:S(2)}) collective-permute-start(f32[2,256,256]{2,1,0:T(8,128)S(1)} %collective-permute-done.prev), channel_id=1, source_target_pairs={{0,1},{1,2},{2,3},{3,0},{4,5},{5,6},{6,7},{7,4},{8,9},{9,10},{10,1... | collective-permute-start | bytes 1572872 | tf_op jit(solution)/shard_map/ppermute | solution.py:317
  18.7 24.4 %collective-permute-start.3 = (f32[2,256,256]{2,1,0:T(8,128)}, f32[2,256,256]{2,1,0:T(8,128)S(1)}, u32[]{:S(2)}, u32[]{:S(2)}) collective-permute-start(f32[2,256,256]{2,1,0:T(8,128)} %bitcast.21), channel_id=1, source_target_pairs={{0,1},{1,2},{2,3},{3,0},{4,5},{5,6},{6,7},{7,4},{8,9},{9,10},{10,1... | collective-permute-start | bytes 1572872 | tf_op jit(solution)/shard_map/ppermute | solution.py:317
  21.8 21.2 %collective-permute-start.5 = (f32[2,256,256]{2,1,0:T(8,128)S(1)}, f32[2,256,256]{2,1,0:T(8,128)S(1)}, u32[]{:S(2)}, u32[]{:S(2)}) collective-permute-start(f32[2,256,256]{2,1,0:T(8,128)S(1)} %collective-permute-done.4.nxt), channel_id=1, source_target_pairs={{0,3},{1,0},{2,1},{3,2},{4,7},{5,4},{6,5},{7,6},{8,11},{9,8},{10,9... | collective-permute-start | bytes 1572872 | tf_op jit(solution)/shard_map/ppermute | solution.py:317
  31.8 1.0 copy-start.1
  32.8 10.2 %copy-start.2 = (f32[1,1,2,256,256]{4,3,2,1,0:T(8,128)S(1)}, f32[1,1,2,256,256]{4,3,2,1,0:T(8,128)}, u32[]{:S(2)}) copy-start(f32[1,1,2,256,256]{4,3,2,1,0:T(8,128)} %param.6) | copy-start | bytes 1572868
  45.7 13.0 %collective-permute-start.7 = (f32[2,256,256]{2,1,0:T(8,128)S(1)}, f32[2,256,256]{2,1,0:T(8,128)S(1)}, u32[]{:S(2)}, u32[]{:S(2)}) collective-permute-start(f32[2,256,256]{2,1,0:T(8,128)S(1)} %get-tuple-element.18.tot_add), channel_id=1, source_target_pairs={{0,4},{4,0},{8,12},{1,5},{5,1},{9,13},{2,6},{6,2},{10,14},{3,7},{7... | collective-permute-start | bytes 1572872 | tf_op jit(solution)/shard_map/ppermute | solution.py:351
  47.0 22.9 %collective-permute-start.6 = (f32[2,256,256]{2,1,0:T(8,128)S(1)}, f32[2,256,256]{2,1,0:T(8,128)S(1)}, u32[]{:S(2)}, u32[]{:S(2)}) collective-permute-start(f32[2,256,256]{2,1,0:T(8,128)S(1)} %get-tuple-element.17.tot_map), channel_id=1, source_target_pairs={{4,0},{8,12},{5,1},{9,13},{6,2},{10,14},{7,3},{11,15},{20,16},{24,... | collective-permute-start | bytes 1572872 | tf_op jit(solution)/shard_map/ppermute | solution.py:345
  71.5 13.3 %collective-permute-start.8 = (f32[2,256,256]{2,1,0:T(8,128)S(1)}, f32[2,256,256]{2,1,0:T(8,128)S(1)}, u32[]{:S(2)}, u32[]{:S(2)}) collective-permute-start(f32[2,256,256]{2,1,0:T(8,128)S(1)} %get-tuple-element.19.joint), channel_id=1, source_target_pairs={{4,8},{0,12},{5,9},{1,13},{6,10},{2,14},{7,11},{3,15},{20,24},{16,... | collective-permute-start | bytes 1572872 | tf_op jit(solution)/shard_map/ppermute | solution.py:356
  84.8 80.0 %copy-start.3 = (bf16[256,384]{1,0:T(8,128)(2,1)S(1)}, bf16[256,384]{1,0:T(8,128)(2,1)}, u32[]{:S(2)}) copy-start(bf16[256,384]{1,0:T(8,128)(2,1)} %constant.19.clone.forward) | copy-start | bytes 589828
  84.8 80.0 %copy-start.4 = (bf16[128,384]{1,0:T(8,128)(2,1)S(1)}, bf16[128,384]{1,0:T(8,128)(2,1)}, u32[]{:S(2)}) copy-start(bf16[128,384]{1,0:T(8,128)(2,1)} %constant.20.clone.backward) | copy-start | bytes 294916
  86.6 7.1 %collective-permute-start.9 = (f32[32,2,8,128]{3,2,1,0:T(8,128)S(1)}, f32[32,2,8,128]{3,2,1,0:T(8,128)S(1)}, u32[]{:S(2)}, u32[]{:S(2)}) collective-permute-start(f32[32,2,8,128]{3,2,1,0:T(8,128)S(1)} %get-tuple-element.23), channel_id=1, source_target_pairs={{0,16},{16,0},{1,17},{17,1},{2,18},{18,2},{3,19},{19,3},{4,20},{20... | collective-permute-start | bytes 786440 | tf_op jit(solution)/shard_map/ppermute | solution.py:368
  164.8 89.4 %copy-start = (f32[1,256,256]{2,1,0:T(8,128)S(1)}, f32[1,256,256]{2,1,0:T(8,128)}, u32[]{:S(2)}) copy-start(f32[1,256,256]{2,1,0:T(8,128)} %param.7) | copy-start | bytes 786436
  167.3 47.0 %all-to-all-start.1 = ((f32[32,32,128]{2,1,0:T(8,128)}), f32[32,32,128]{2,1,0:T(8,128)S(1)}, u32[]{:S(2)}, u32[]{:S(2)}) async-start(f32[32,32,128]{2,1,0:T(8,128)} %bitcast.6), calls=%async_computation.1 | async-start | bytes 1048576 | tf_op jit(solution)/shard_map/all_to_all | solution.py:377
  214.3 40.2 %collective-permute-start.10 = (f32[32,2,8,128]{3,2,1,0:T(8,128)S(1)}, f32[32,2,8,128]{3,2,1,0:T(8,128)S(1)}, u32[]{:S(2)}, u32[]{:S(2)}) collective-permute-start(f32[32,2,8,128]{3,2,1,0:T(8,128)S(1)} %dynamic-slice_bitcast_fusion), channel_id=1, source_target_pairs={{0,16},{16,0},{1,17},{17,1},{2,18},{18,2},{3,19},{19,3},{4,20},{20... | collective-permute-start | bytes 786440 | tf_op jit(solution)/shard_map/ppermute | solution.py:380
